TPU v7x, 256 devices: a whole 4x4x8 slice. The times are simulated.
256 devices in a mesh: seq: 32 (over z, x), exp: 8 (over y, core).
Axes of the slice: x: 4, y: 4, z: 8, core: 2. Of those that a mesh axis runs over, the one named last changes fastest.
Arguments:
- tokens: bfloat16 [32768, 2560], P(('seq', 'exp')), may hold values from -6 to 6
- routes: int32 [32768, 1], P(('seq', 'exp')), may hold values from 0 to 15; in each aligned block of 128 rows (0 to 127, 128 to 255, ...) at most 16 rows name the same one
- gate_inner_weight: bfloat16 [2560, 2, 3072], P(None, None, 'exp'), may hold values from -0.125 to 0.125
- state_map_weight: bfloat16 [2560, 256], replicated, may hold values from -0.125 to 0.125
- step_size_weight: bfloat16 [2560, 48], P(None, 'exp'), may hold values from -0.125 to 0.125
- adapter_down_weight: bfloat16 [2560, 128], P(None, 'exp'), may hold values from -0.125 to 0.125
- adapter_up_weight: bfloat16 [128, 2, 3072], P(None, None, 'exp'), may hold values from -1.5 to 1.5
- inner_conv_taps: float32 [4, 3072], P(None, 'exp'), may hold values from -3 to 3
- state_map_taps: float32 [4, 256], replicated, may hold values from -3 to 3
- inner_conv_bias: float32 [3072], P('exp'), may hold values from -3 to 3
- state_map_conv_bias: float32 [256], replicated, may hold values from -3 to 3
- step_size_bias: float32 [48], P('exp'), may hold values from -6 to -3
- head_decay_rate: float32 [48], P('exp'), may hold values from 4.656613e-06 to 8
- direct_head_scale: float32 [48], P('exp'), may hold values from 0.5 to 2
- gated_norm_scale: float32 [3072], P('exp'), may hold values from 0.5 to 1.5
Outputs:
- mixed: bfloat16 [32768, 3072], P('seq', 'exp')
Inputs may be any that keep to these rules, and one draw needn't show every extreme that they name: `routes`: among the rows of one device no expert is named more than 16 times.
All inputs are finite; a program needn't handle non-finite values.
Results may differ from a plain program's by a relative error of at most 0.0034.
Values may be sent and summed in bfloat16 or wider, within the bound.
A program may use at most 64 MiB of HBM per device.

v0:
```python
import jax
import jax.numpy as jnp
from jax import lax
from jax.sharding import Mesh
from jax.sharding import PartitionSpec as P

STATE = 128
HEADDIM = 64
ADAPTER_EXPERTS = 16
EXPERT_RANK = 8
GROUP = 256
INNER_WIDTH = 3072
SEQ = ("seq_0", "seq_1")
SEQ_EXP = ("seq_0", "seq_1", "exp")


HIGH = lax.Precision.HIGHEST


def laid_out(parts, dim):
    lengths = list(parts.shape[1:])
    lengths[dim] *= parts.shape[0]
    return jnp.moveaxis(parts, 0, dim).reshape(lengths)


def copy_for_each(value, axis):
    size = lax.axis_size(axis)
    return lax.all_to_all(
        jnp.broadcast_to(value[None], (size, *value.shape)), axis, 0, 0, tiled=True
    )


def gathered_copies(value, axis, dim):
    return laid_out(copy_for_each(value, axis), dim)


def passed_along(block, axis, distance):
    devices = range(lax.axis_size(axis))
    route = [(i - distance, i) for i in devices if i - distance in devices]
    return lax.ppermute(block, axis, route)


def filled_with(value, identity):
    return jax.tree.map(
        lambda a, e: jnp.broadcast_to(jnp.asarray(e, a.dtype), a.shape), value, identity
    )


def entering_2(value, axes, combine, identity):
    before = start = filled_with(value, identity)
    running = value
    for axis in reversed(axes):
        size, index = (lax.axis_size(axis), lax.axis_index(axis))
        pieces = jax.tree.map(lambda part: lax.all_gather(part, axis), running)
        inside, running = (start, start)
        for k in range(size):
            passed = k < index
            running = combine(running, jax.tree.map(lambda part: part[k], pieces))
            inside = jax.tree.map(lambda new, old: jnp.where(passed, new, old), running, inside)
        before = combine(inside, before)
    return before


def taken_together(value, axis):
    return copy_for_each(value, axis).sum(axis=0)


def block_step(state, items):
    inner, bmap, cmap, step, decay = items
    cumul = jnp.cumsum(decay, axis=0)
    length = decay.shape[0]
    rows = lax.broadcasted_iota(jnp.int32, (length, length), 0)
    cols = lax.broadcasted_iota(jnp.int32, (length, length), 1)
    causal = (rows >= cols)[:, :, None]
    differ = jnp.where(causal, cumul[:, None, :] - cumul[None, :, :], 0.0)
    segment = jnp.where(causal, jnp.exp(differ), 0.0)
    gram = jnp.dot(cmap, bmap.T, precision=HIGH)
    weights = gram[:, :, None] * segment * step[None, :, :]
    output = jnp.einsum("ijh,jhp->ihp", weights, inner, precision=HIGH)
    output = output + jnp.exp(cumul)[:, :, None] * jnp.einsum(
        "in,hnp->ihp", cmap, state, precision=HIGH
    )
    final = cumul[-1]
    carried = jnp.exp(final[None, :] - cumul) * step
    update = jnp.einsum("jn,jhp->hnp", bmap, carried[:, :, None] * inner, precision=HIGH)
    return (jnp.exp(final)[:, None, None] * state + update, output)


def run_blocks(inner, bmap, cmap, step, decay, state, block):
    total = inner.shape[0]
    count_blocks = total // block
    items = (
        inner.reshape(count_blocks, block, inner.shape[1], inner.shape[2]),
        bmap.reshape(count_blocks, block, bmap.shape[1]),
        cmap.reshape(count_blocks, block, cmap.shape[1]),
        step.reshape(count_blocks, block, step.shape[1]),
        decay.reshape(count_blocks, block, decay.shape[1]),
    )
    final, output = lax.scan(block_step, state, items)
    return (final, output.reshape(total, inner.shape[1], inner.shape[2]))


def causal_conv(extended, weights, bias):
    length = extended.shape[0] - weights.shape[0] + 1
    output = bias[None, :] + jnp.zeros((length, weights.shape[1]), jnp.float32)
    for shift_idx in range(weights.shape[0]):
        output = output + weights[shift_idx][None, :] * extended[shift_idx : shift_idx + length]
    return jax.nn.silu(output)


def pick_ranks(partial_columns, route, experts, width):
    column_expert = lax.broadcasted_iota(jnp.int32, (experts * width,), 0) // width
    masked = jnp.where(route[:, None] == column_expert[None, :], partial_columns, 0.0)
    return jnp.sum(masked.reshape(partial_columns.shape[0], experts, width), axis=1)


def lift_ranks(ranks, route, experts):
    width = ranks.shape[1]
    column_expert = lax.broadcasted_iota(jnp.int32, (experts * width,), 0) // width
    repeated_tiles = jnp.tile(ranks, (1, experts))
    return jnp.where(
        route[:, None] == column_expert[None, :], repeated_tiles, jnp.zeros_like(repeated_tiles)
    )


def body(
    tokens,
    routes,
    gate_inner_weight,
    state_map_weight,
    step_size_weight,
    adapter_down_weight,
    adapter_up_weight,
    inner_conv_taps,
    state_map_taps,
    inner_conv_bias,
    state_map_conv_bias,
    step_size_bias,
    head_decay_rate,
    direct_head_scale,
    gated_norm_scale,
):
    whole, route_all = (
        lax.all_gather(tokens, "exp", axis=0, tiled=True),
        lax.all_gather(routes, "exp", axis=0, tiled=True),
    )
    route_flat = route_all[:, 0]
    all_down_maps = gathered_copies(adapter_down_weight, "exp", 1)
    partial_columns = jnp.dot(whole, all_down_maps, preferred_element_type=jnp.float32)
    ranks = pick_ranks(partial_columns, route_flat, ADAPTER_EXPERTS, EXPERT_RANK).astype(
        jnp.bfloat16
    )
    length = whole.shape[0]
    features = whole.shape[1]
    split_widths = gate_inner_weight.shape[2]
    raised_values = lift_ranks(ranks, route_flat, ADAPTER_EXPERTS)
    gate_inner_values = jnp.dot(
        whole,
        gate_inner_weight.reshape(features, 2 * split_widths),
        preferred_element_type=jnp.float32,
    )
    gate_inner_values = gate_inner_values + jnp.dot(
        raised_values,
        adapter_up_weight.reshape(ADAPTER_EXPERTS * EXPERT_RANK, 2 * split_widths),
        preferred_element_type=jnp.float32,
    )
    gate = gate_inner_values[:, :split_widths]
    inner = gate_inner_values[:, split_widths:]
    bc_raw = jnp.dot(whole, state_map_weight, preferred_element_type=jnp.float32)
    dt_raw = jnp.dot(whole, step_size_weight, preferred_element_type=jnp.float32)
    margin = inner_conv_taps.shape[0] - 1
    inner_rim, bc_rim = passed_along((inner[length - margin :], bc_raw[length - margin :]), SEQ, 1)
    xconv = causal_conv(
        jnp.concatenate([inner_rim, inner], axis=0), inner_conv_taps, inner_conv_bias
    )
    bconv = causal_conv(
        jnp.concatenate([bc_rim, bc_raw], axis=0), state_map_taps, state_map_conv_bias
    )
    bmap = bconv[:, :STATE]
    cmap = bconv[:, STATE:]
    step = jax.nn.softplus(dt_raw + step_size_bias[None, :])
    decay = -head_decay_rate[None, :] * step
    heads = head_decay_rate.shape[0]
    heads_in = xconv.reshape(length, heads, HEADDIM)
    empty_state = jnp.zeros((heads, STATE, HEADDIM), jnp.float32)
    final, output = run_blocks(heads_in, bmap, cmap, step, decay, empty_state, GROUP)
    factor = jnp.exp(jnp.sum(decay, axis=0))

    def combine(earlier, later):
        return (earlier[0] * later[0], later[0][:, None, None] * earlier[1] + later[1])

    total_decay, entering = entering_2(
        (factor, final), SEQ, combine, (jnp.ones((heads,), jnp.float32), empty_state)
    )
    cumul = jnp.cumsum(decay, axis=0)
    output = output + jnp.exp(cumul)[:, :, None] * jnp.einsum(
        "in,hnp->ihp", cmap, entering, precision=HIGH
    )
    output = output + direct_head_scale[None, :, None] * heads_in
    gated = output.reshape(length, split_widths) * jax.nn.silu(gate)
    squares = taken_together(jnp.sum(gated * gated, axis=1), "exp")
    scale = lax.rsqrt(squares / INNER_WIDTH + 1e-05)
    return (gated * scale[:, None] * gated_norm_scale[None, :]).astype(jnp.bfloat16)


def solution(mesh):
    split = Mesh(mesh.devices.reshape(8, 4, mesh.shape["exp"]), ("seq_0", "seq_1", "exp"))
    in_specs = (
        P(SEQ_EXP, None),
        P(SEQ_EXP, None),
        P(None, None, "exp"),
        P(),
        P(None, "exp"),
        P(None, "exp"),
        P(None, None, "exp"),
        P(None, "exp"),
        P(),
        P("exp"),
        P(),
        P("exp"),
        P("exp"),
        P("exp"),
        P("exp"),
    )
    out_specs = P(SEQ, "exp")
    return jax.shard_map(body, mesh=split, in_specs=in_specs, out_specs=out_specs, check_vma=False)
```

profile of v0, /device:TPU:1, one launch (start us, length us, event | category | flops | bytes accessed | tf_op | source)
XLA Modules:
  0.0 258.2 jit_solution(6099084624724914850)
XLA Ops:
  7.3 1.8 broadcast_in_dim.72
  9.0 6.6 %all-to-all-start = ((bf16[8,2560,16]{1,2,0:T(8,128)(2,1)}), bf16[8,2560,16]{1,2,0:T(8,128)(2,1)S(1)}, u32[]{:S(2)}, u32[]{:S(2)}) async-start(bf16[8,2560,16]{1,2,0:T(8,128)(2,1)} %broadcast_in_dim.72), calls=%async_computation | async-start | bytes 1310720 | tf_op jit(solution)/shard_map/all_to_all | solution.py:28
  15.7 4.8 %copy.123 = bf16[320,8,2,384]{3,1,2,0:T(8,128)(2,1)} copy(bf16[320,8,2,384]{3,2,1,0:T(2,128)(2,1)} %bitcast.267) | data formatting | bytes 7864320
  21.8 11.0 %all_gather.25 = s32[1024,1]{0,1:T(1,128)S(1)} all-gather(s32[128,1]{0,1:T(1,128)S(1)} %copy-done.18), channel_id=1, replica_groups=mesh['seq_0'=8,'seq_1'=4,'exp'=8] {'exp'}, dimensions={0}, use_global_device_ids=true | all-gather | bytes 4608 | tf_op jit(solution)/shard_map/all_gather | solution.py:145
  32.9 19.5 %all-gather.6.cloned.1.call-done = bf16[1024,2560]{1,0:T(8,128)(2,1)} async-done(((bf16[128,2560]{1,0:T(8,128)(2,1)}), bf16[1024,2560]{1,0:T(8,128)(2,1)}) %all-gather.6.cloned.1.call-update) | async-done | bytes 5242896 | tf_op jit(solution)/shard_map/all_gather | solution.py:144
  52.4 9.5 %fusion.98 = f32[1024,768]{1,0:T(8,128)} fusion(bf16[1024,2560]{1,0:T(8,128)(2,1)} %all-gather.6.cloned.1.call-done, bf16[2560,768]{1,0:T(8,128)(2,1)} %bitcast.268), kind=kOutput, calls=%fused_computation.167 | convolution fusion | flops 4026531840 | bytes 12320768 | tf_op jit(solution)/shard_map/dot_general | solution.py:157
  61.9 4.4 %fusion.54 = bf16[1024,8]{0,1:T(8,128)(2,1)S(1)} fusion(bf16[1024,2560]{1,0:T(8,128)(2,1)} %all-gather.6.cloned.1.call-done, bf16[2560,128]{0,1:T(8,128)(2,1)S(1)} %bitcast.271, s32[1024]{0:T(1024)S(1)} %bitcast.281, s32[128]{0:T(128)S(1)} %and_select_fusion), kind=kOutput, calls=%fused_computation.70 | convolution fusion | flops 671473664 | bytes 5919232 | tf_op jit(solution)/shard_map/dot_general | solution.py:149
  67.1 1.6 copy-done.3
  68.8 3.2 %collective-permute-start = (f32[3,384]{1,0:T(4,128)S(1)}, f32[3,384]{1,0:T(4,128)S(1)}, u32[]{:S(2)}, u32[]{:S(2)}) collective-permute-start(f32[3,384]{1,0:T(4,128)S(1)} %slice.215), channel_id=1, source_target_pairs={{0,8},{8,16},{16,24},{24,32},{32,40},{40,48},{48,56},{56,64},{64,7... | collective-permute-start | bytes 13832 | tf_op jit(solution)/shard_map/ppermute | solution.py:40
  72.0 1.5 fusion.99
  73.6 3.1 %collective-permute-start.1 = (f32[3,256]{1,0:T(4,128)S(1)}, f32[3,256]{1,0:T(4,128)S(1)}, u32[]{:S(2)}, u32[]{:S(2)}) collective-permute-start(f32[3,256]{1,0:T(4,128)S(1)} %slice.221), channel_id=1, source_target_pairs={{0,8},{8,16},{16,24},{24,32},{32,40},{40,48},{48,56},{56,64},{64,7... | collective-permute-start | bytes 9224 | tf_op jit(solution)/shard_map/ppermute | solution.py:40
  76.7 1.6 fusion.95
  78.4 8.6 %all-reduce = f32[24]{0:T(128)S(1)} all-reduce(f32[24]{0:T(128)S(1)} %exponential_dynamic-update-slice_fusion), channel_id=2, replica_groups=mesh['seq_0'=8,'seq_1'=4,'exp'=8] {'seq_1'}, use_global_device_ids=true, to_apply=%add | all-reduce | flops 24 | bytes 192
  91.2 2.2 divide_multiply_fusion
  93.4 1.9 copy.104
  95.3 1.9 reshape_reshape.3
  97.2 81.9 %while.13 = (s32[]{:T(128)}, f32[6,128,64]{1,2,0:T(8,128)S(1)}, f32[4,256,6,64]{1,0,3,2:T(4,128)}, f32[4,256,6]{1,2,0:T(8,128)S(1)}, f32[4,256,6]{1,2,0:T(8,128)...) while((s32[]{:T(128)}, f32[6,128,64]{1,2,0:T(8,128)S(1)}, ...), condition=%wide.region_4.5_spmd.clone, body=%wide.region_1.4_spmd.clone.sunk | while | flops 707316736 | bytes 6607687 | solution.py:99
  97.2 1.8 reduce-window.26
  99.7 1.4 fusion.133
  102.5 1.8 constant_dynamic-slice_fusion.2
  104.3 2.0 fusion.134
  106.7 9.5 %dynamic_update_slice.6 = f32[4,256,6,64]{1,0,3,2:T(4,128)} dynamic-update-slice(f32[4,256,6,64]{1,0,3,2:T(4,128)} %get-tuple-element.250, f32[1,256,6,64]{1,0,3,2:T(1,128)S(1)} %copy.158, s32[]{:T(128)} %get-tuple-element.248, s32[]{:T(128)} %constant.71.clone.1..sunk, s32[]{:T(128)} %constant.71.clone.1..sunk, s32[]{:T(128)} %constant.71.clone.1..sunk) | dynamic-update-slice | bytes 786436 | tf_op jit(solution)/shard_map/while/body/jit(dynamic_update_index_in_dim)/dynamic_update_slice | solution.py:99
  117.7 1.8 reduce-window.26
  120.2 1.4 fusion.133
  122.9 1.8 constant_dynamic-slice_fusion.2
  124.8 2.0 fusion.134
  127.2 9.5 %dynamic_update_slice.6 = f32[4,256,6,64]{1,0,3,2:T(4,128)} dynamic-update-slice(f32[4,256,6,64]{1,0,3,2:T(4,128)} %get-tuple-element.250, f32[1,256,6,64]{1,0,3,2:T(1,128)S(1)} %copy.158, s32[]{:T(128)} %get-tuple-element.248, s32[]{:T(128)} %constant.71.clone.1..sunk, s32[]{:T(128)} %constant.71.clone.1..sunk, s32[]{:T(128)} %constant.71.clone.1..sunk) | dynamic-update-slice | bytes 786436 | tf_op jit(solution)/shard_map/while/body/jit(dynamic_update_index_in_dim)/dynamic_update_slice | solution.py:99
  138.1 1.8 reduce-window.26
  140.7 1.4 fusion.133
  143.4 1.8 constant_dynamic-slice_fusion.2
  145.3 2.0 fusion.134
  147.7 9.5 %dynamic_update_slice.6 = f32[4,256,6,64]{1,0,3,2:T(4,128)} dynamic-update-slice(f32[4,256,6,64]{1,0,3,2:T(4,128)} %get-tuple-element.250, f32[1,256,6,64]{1,0,3,2:T(1,128)S(1)} %copy.158, s32[]{:T(128)} %get-tuple-element.248, s32[]{:T(128)} %constant.71.clone.1..sunk, s32[]{:T(128)} %constant.71.clone.1..sunk, s32[]{:T(128)} %constant.71.clone.1..sunk) | dynamic-update-slice | bytes 786436 | tf_op jit(solution)/shard_map/while/body/jit(dynamic_update_index_in_dim)/dynamic_update_slice | solution.py:99
  157.2 1.4 fusion.131
  158.6 1.8 reduce-window.26
  161.1 1.4 fusion.133
  163.9 1.8 constant_dynamic-slice_fusion.2
  165.7 2.0 fusion.134
  168.1 9.5 %dynamic_update_slice.6 = f32[4,256,6,64]{1,0,3,2:T(4,128)} dynamic-update-slice(f32[4,256,6,64]{1,0,3,2:T(4,128)} %get-tuple-element.250, f32[1,256,6,64]{1,0,3,2:T(1,128)S(1)} %copy.158, s32[]{:T(128)} %get-tuple-element.248, s32[]{:T(128)} %constant.71.clone.1..sunk, s32[]{:T(128)} %constant.71.clone.1..sunk, s32[]{:T(128)} %constant.71.clone.1..sunk) | dynamic-update-slice | bytes 786436 | tf_op jit(solution)/shard_map/while/body/jit(dynamic_update_index_in_dim)/dynamic_update_slice | solution.py:99
  179.0 11.5 %all-gather.1 = f32[24,128,64]{1,2,0:T(8,128)S(1)} all-gather(f32[6,128,64]{1,2,0:T(8,128)S(1)} %get-tuple-element.49), channel_id=3, replica_groups=mesh['seq_0'=8,'seq_1'=4,'exp'=8] {'seq_1'}, dimensions={0}, use_global_device_ids=true | all-gather | bytes 983040 | tf_op jit(solution)/shard_map/all_gather | solution.py:54
  191.5 1.7 reduce-window.16
  193.6 12.4 %all-gather.2 = f32[8,1,6]{2,1,0:T(1,128)S(1)} all-gather(f32[1,1,6]{2,1,0:T(1,128)S(1)} %get-tuple-element.177), channel_id=1, replica_groups=mesh['seq_0'=8,'seq_1'=4,'exp'=8] {'seq_0'}, dimensions={0}, use_global_device_ids=true | all-gather | bytes 216 | tf_op jit(solution)/shard_map/all_gather | solution.py:54
  206.0 2.9 %reshape.225 = f32[1024,6,64]{0,2,1:T(8,128)} reshape(f32[4,256,6,64]{1,0,3,2:T(4,128)} %get-tuple-element.48) | data formatting | bytes 3145728 | tf_op jit(solution)/shard_map/reshape | solution.py:100
  208.9 19.9 %all-gather.8.cloned.1.call-done = f32[8,6,128,64]{2,3,1,0:T(8,128)} async-done(((f32[1,6,128,64]{2,3,1,0:T(8,128)}), f32[8,6,128,64]{2,3,1,0:T(8,128)}) %all-gather.8.cloned.1.call-update) | async-done | bytes 1572880 | tf_op jit(solution)/shard_map/all_gather | solution.py:54
  228.8 2.0 fusion.71
  230.8 1.4 fusion.93
  232.8 1.6 copy.110
  234.5 2.5 multiply_reduce_fusion
  236.9 13.3 %all_to_all.11 = f32[8,1,1024]{2,1,0:T(1,128)S(1)} all-to-all(f32[8,1,1024]{2,1,0:T(1,128)S(1)} %broadcast_in_dim.77), channel_id=1, replica_groups=mesh['seq_0'=8,'seq_1'=4,'exp'=8] {'exp'}, dimensions={0} | all-to-all | bytes 65536 | tf_op jit(solution)/shard_map/all_to_all | solution.py:28
  (147 shorter events, 23.5 us)
Async XLA Ops:
  6.5 65.5 %copy-start = (bf16[2560,256]{1,0:T(8,128)(2,1)S(1)}, bf16[2560,256]{1,0:T(8,128)(2,1)}, u32[]{:S(2)}) copy-start(bf16[2560,256]{1,0:T(8,128)(2,1)} %param.20) | copy-start | bytes 3932164
  6.5 45.9 %all-gather.6.cloned.1.call-start = ((), (), s32[]{:S(2)}) async-start(), calls=%async_computation.2 | async-start | bytes 5898240 | tf_op jit(solution)/shard_map/all_gather | solution.py:144
  9.0 52.9 %all-to-all-start = ((bf16[8,2560,16]{1,2,0:T(8,128)(2,1)}), bf16[8,2560,16]{1,2,0:T(8,128)(2,1)S(1)}, u32[]{:S(2)}, u32[]{:S(2)}) async-start(bf16[8,2560,16]{1,2,0:T(8,128)(2,1)} %broadcast_in_dim.72), calls=%async_computation | async-start | bytes 1310720 | tf_op jit(solution)/shard_map/all_to_all | solution.py:28
  15.7 213.2 %all-gather.8.cloned.1.call-start = ((), (), s32[]{:S(2)}) async-start(), calls=%async_computation.3 | async-start | bytes 1769472 | tf_op jit(solution)/shard_map/all_gather | solution.py:54
  15.7 4.9 %copy-start.9 = (bf16[128,2,384]{2,1,0:T(2,128)(2,1)S(1)}, bf16[128,2,384]{2,1,0:T(2,128)(2,1)}, u32[]{:S(2)}) copy-start(bf16[128,2,384]{2,1,0:T(2,128)(2,1)} %param.23) | copy-start | bytes 589828
  15.7 4.9 %copy-start.19 = (f32[6]{0:T(128)S(1)}, f32[6]{0:T(128)}, u32[]{:S(2)}) copy-start(f32[6]{0:T(128)} %param.29) | copy-start | bytes 76
  15.7 5.0 %copy-start.20 = (u32[256]{0:T(256)S(1)}, u32[256]{0:T(256)}, u32[]{:S(2)}) copy-start(u32[256]{0:T(256)} %constant.97) | copy-start | bytes 3076
  15.7 6.1 %copy-start.18 = (s32[128,1]{0,1:T(1,128)S(1)}, s32[128,1]{0,1:T(1,128)}, u32[]{:S(2)}) copy-start(s32[128,1]{0,1:T(1,128)} %param.18) | copy-start | bytes 1540
  15.7 17.1 %copy-start.11 = (f32[4,384]{1,0:T(4,128)S(1)}, f32[4,384]{1,0:T(4,128)}, u32[]{:S(2)}) copy-start(f32[4,384]{1,0:T(4,128)} %param.24) | copy-start | bytes 18436
  15.7 17.1 %copy-start.12 = (f32[4,256]{1,0:T(4,128)S(1)}, f32[4,256]{1,0:T(4,128)}, u32[]{:S(2)}) copy-start(f32[4,256]{1,0:T(4,128)} %param.25) | copy-start | bytes 12292
  61.9 4.4 %copy-start.8 = (f32[1024,768]{1,0:T(8,128)S(1)}, f32[1024,768]{1,0:T(8,128)}, u32[]{:S(2)}) copy-start(f32[1024,768]{1,0:T(8,128)} %fusion.98) | copy-start | bytes 9437188
  66.4 5.6 %copy-start.4 = (bf16[1024,2560]{1,0:T(8,128)(2,1)S(1)}, bf16[1024,2560]{1,0:T(8,128)(2,1)}, u32[]{:S(2)}) copy-start(bf16[1024,2560]{1,0:T(8,128)(2,1)} %all-gather.6.cloned.1.call-done) | copy-start | bytes 15728644
  67.1 1.7 copy-start.3
  68.8 7.9 %copy-start.10 = (bf16[2560,6]{0,1:T(8,128)(2,1)S(1)}, bf16[2560,6]{0,1:T(8,128)(2,1)}, u32[]{:S(2)}) copy-start(bf16[2560,6]{0,1:T(8,128)(2,1)} %param.21) | copy-start | bytes 92164
  68.8 7.9 %copy-start.14 = (f32[6]{0:T(128)S(1)}, f32[6]{0:T(128)}, u32[]{:S(2)}) copy-start(f32[6]{0:T(128)} %param.28) | copy-start | bytes 76
  68.8 21.7 %collective-permute-start = (f32[3,384]{1,0:T(4,128)S(1)}, f32[3,384]{1,0:T(4,128)S(1)}, u32[]{:S(2)}, u32[]{:S(2)}) collective-permute-start(f32[3,384]{1,0:T(4,128)S(1)} %slice.215), channel_id=1, source_target_pairs={{0,8},{8,16},{16,24},{24,32},{32,40},{40,48},{48,56},{56,64},{64,7... | collective-permute-start | bytes 13832 | tf_op jit(solution)/shard_map/ppermute | solution.py:40
  73.6 13.5 %collective-permute-start.1 = (f32[3,256]{1,0:T(4,128)S(1)}, f32[3,256]{1,0:T(4,128)S(1)}, u32[]{:S(2)}, u32[]{:S(2)}) collective-permute-start(f32[3,256]{1,0:T(4,128)S(1)} %slice.221), channel_id=1, source_target_pairs={{0,8},{8,16},{16,24},{24,32},{32,40},{40,48},{48,56},{56,64},{64,7... | collective-permute-start | bytes 9224 | tf_op jit(solution)/shard_map/ppermute | solution.py:40
  87.1 0.7 copy-start.16
  88.4 1.0 copy-start.5
  89.4 1.8 slice-start
  89.4 1.8 copy-start.13
  95.3 1.9 copy-start.1
  208.9 21.9 %copy-start.6 = (f32[1024,256]{1,0:T(8,128)S(1)}, f32[1024,256]{1,0:T(8,128)}, u32[]{:S(2)}) copy-start(f32[1024,256]{1,0:T(8,128)} %copy-done.5) | copy-start | bytes 3145732
  228.8 3.4 %copy-start.7 = (f32[1024,6,64]{0,2,1:T(8,128)S(1)}, f32[1024,6,64]{0,2,1:T(8,128)}, u32[]{:S(2)}) copy-start(f32[1024,6,64]{0,2,1:T(8,128)} %reshape.225) | copy-start | bytes 4718596
  230.8 1.5 copy-start.2
  230.8 1.5 copy-start.17
  234.5 15.8 %copy-start.15 = (f32[384]{0:T(512)S(1)}, f32[384]{0:T(512)}, u32[]{:S(2)}) copy-start(f32[384]{0:T(512)} %param.31) | copy-start | bytes 4612
Sparse Core Ops, SparseCore 0:
  9.2 43.2 all-gather.5
  191.5 37.2 all-gather.7
where the time goes:
time: 260 us; the launch traced here: 258 us
  local copies, waits for them, and re-layouts  69.9 us (27%)
  blocking collectives  56.9 us (22%)
  matrix products  43.5 us (17%)
  waiting for transfers between devices  40.2 us (15%)
  other arithmetic  20.2 us (8%)
  between operations  14.4 us (6%)
  starting transfers between devices  13 us (5%)
    dynamic_update_slice x8, local copies, waits for them, and re-layouts, run_blocks(): final, output = lax.scan(block_step, state, items)  39.7 us
    all_gather x2, blocking collectives, entering_2(): pieces = jax.tree.map(lambda part: lax.all_gather(part, axis), running)  23.9 us
    all_gather x1, waiting for transfers between devices, entering_2(): pieces = jax.tree.map(lambda part: lax.all_gather(part, axis), running)  19.9 us
    all_gather x1, waiting for transfers between devices, body(): lax.all_gather(tokens, 'exp', axis=0, tiled=True)  19.5 us
    all_to_all x1, blocking collectives, copy_for_each(): lax.all_to_all(jnp.broadcast_to(value[None], (size, *value.shape)), axis,...  13.3 us
    all_gather x1, blocking collectives, body(): lax.all_gather(routes, 'exp', axis=0, tiled=True)  11 us
    dot_general x1, matrix products, body(): jnp.dot(whole, gate_inner_weight.reshape(features, 2 * split_widths), pre...  9.51 us
    another operation x10, other arithmetic  9.32 us
  transfers between devices with their start and end apart: 5, of which 2 were waited for; matrix products, arithmetic and copies ran while one was open for 10% of the time, Pallas kernels for 0%

commit v1 on v0

v1 whole, which is shorter than its diff:
```python
import functools

import jax
import jax.numpy as jnp
from jax import lax
from jax.experimental import pallas as pl
from jax.experimental.pallas import tpu as pltpu
from jax.sharding import PartitionSpec as P

MODEL = 2560
STATE = 128
HEADS = 6
COLS = 384
RANK = 8
BLOCK = 128
N_EXP = 8
N_SEQ = 32
ROWS = 1024
INNER_WIDTH = 3072
SEG = 144
PIECES = ((128, 16), (0, 32), (32, 32), (64, 32), (96, 32))
F32, BF16 = jnp.float32, jnp.bfloat16
NT = (((1,), (1,)), ((), ()))
NN = (((1,), (0,)), ((), ()))


def dot(a, b, dims=NN):
    return lax.dot_general(a, b, dims, preferred_element_type=F32)


def split(a):
    hi = a.astype(BF16)
    return hi, (a - hi.astype(F32)).astype(BF16)


def dot3(a, b, dims=NN):
    (ah, al), (bh, bl) = a, b
    return dot(ah, bh, dims) + (dot(ah, bl, dims) + dot(al, bh, dims))


def silu(v):
    return v / (1.0 + jnp.exp(-v))


def lane_row(ref, width):
    lane = lax.broadcasted_iota(jnp.int32, (1, 128 if width == 1 else HEADS * width), 1) // width
    row = jnp.zeros(lane.shape, F32)
    for h in range(HEADS):
        row = jnp.where(lane == h, ref[h], row)
    return row


def kernel(
    tok_hbm, routes_ref, wgi_hbm, wbc_hbm, dt_ref, down_hbm, up_ref,
    taps_ref, btaps_ref, bias_ref, bbias_ref, sbias_ref, rate_ref, direct_ref, norm_ref,
    out_ref,
    tall, routes, wgi, wbc, ddt, zg, zi, zb, sd, rimx, rimb,
    cc, ybuf, ec, f1, r1, o2, r2, ebuf, sq, r3, scl,
    lsem, rsem, ssem, fsem, csem, rtr, rts, rimr, rims, s1, v1, s2, v2, s3, v3,
):
    e, s = lax.axis_index("exp"), lax.axis_index("seq")
    y, c = e // 2, e % 2
    yp, ym, yo = (y + 1) % 4, (y + 3) % 4, (y + 2) % 4
    plus, minus, mate = yp * 2 + c, ym * 2 + c, y * 2 + 1 - c

    loads = [
        pltpu.make_async_copy(tok_hbm, tall.at[e, pl.ds(0, 128)], lsem.at[0]),
        pltpu.make_async_copy(down_hbm, tall.at[e, pl.ds(128, 16)], lsem.at[1]),
        pltpu.make_async_copy(wgi_hbm, wgi, lsem.at[2]),
        pltpu.make_async_copy(wbc_hbm, wbc, lsem.at[3]),
    ]
    for load in loads:
        load.start()

    barrier = pltpu.get_barrier_semaphore()
    for d in range(1, N_EXP):
        pl.semaphore_signal(barrier, inc=1, device_id={"exp": (e + d) % N_EXP})

    @pl.loop(1, N_SEQ)
    def _(d):
        pl.semaphore_signal(barrier, inc=1, device_id={"seq": (s + d) % N_SEQ})

    routes[e] = routes_ref[...]
    ddt[...] = jnp.zeros_like(ddt)
    ddt[pl.ds(128, HEADS), :] = dt_ref[...]
    loads[0].wait()
    loads[1].wait()
    pl.semaphore_wait(barrier, N_EXP - 1 + N_SEQ - 1)

    def piece(b, k):
        first, size = PIECES[k]
        return tall.at[b, pl.ds(first, size)]

    def push(b, k, to, sem):
        copy = pltpu.make_async_remote_copy(
            src_ref=piece(b, k), dst_ref=piece(b, k), send_sem=sem, recv_sem=rsem.at[b, k],
            device_id={"exp": to},
        )
        copy.start()
        sent.append(copy)

    def landed(b, k):
        pltpu.make_async_remote_copy(
            src_ref=piece(b, k), dst_ref=piece(b, k), send_sem=lsem.at[0], recv_sem=rsem.at[b, k],
            device_id={"exp": mate},
        ).wait_recv()

    sent = []
    for d in range(1, N_EXP):
        copy = pltpu.make_async_remote_copy(
            src_ref=routes_ref, dst_ref=routes.at[e], send_sem=rts.at[d], recv_sem=rtr.at[e],
            device_id={"exp": (e + d) % N_EXP},
        )
        copy.start()
        sent.append(copy)
    for k, j in zip((0, 1, 2, 3, 4), (0, 3, 4, 1, 2)):
        push(e, k, plus, ssem.at[0, k])
        push(e, j, minus, ssem.at[1, j])
        push(e, k, mate, ssem.at[2, k])

    def take(b, k, slot, forward=None):
        landed(b, k)
        if forward is not None:
            push(b, k, forward, fsem.at[k])
        push(b, k, mate, csem.at[slot, k])

    bm, bp, bo = ym * 2 + c, yp * 2 + c, yo * 2 + c
    take(bm, 0, 0, plus)
    take(bp, 0, 1)
    take(bo, 0, 2)
    others = [y * 2 + 1 - c, ym * 2 + 1 - c, yp * 2 + 1 - c, yo * 2 + 1 - c]
    for b in others:
        landed(b, 0)
    for d in range(1, N_EXP):
        b = (e + d) % N_EXP
        pltpu.make_async_remote_copy(
            src_ref=routes_ref, dst_ref=routes.at[b], send_sem=lsem.at[0], recv_sem=rtr.at[b],
            device_id={"exp": mate},
        ).wait_recv()
    for b in range(N_EXP):
        ddt[pl.ds(16 * b, 16), :] = tall[b, pl.ds(128, 16), :]
    loads[2].wait()
    loads[3].wait()

    expert_of_lane = lax.broadcasted_iota(jnp.int32, (BLOCK, 128), 1) // RANK

    def project(b):
        t = tall[b, pl.ds(0, BLOCK), :]
        row = pl.multiple_of(b * BLOCK, BLOCK)
        aux = dot(t, ddt[...], NT)
        sd[pl.ds(row, BLOCK), :] = aux[:, 128:]
        route = jnp.broadcast_to(routes[b].astype(F32), (BLOCK, 128)).T.astype(jnp.int32)
        lifted = jnp.where(route == expert_of_lane, aux[:, :128], 0.0).astype(BF16)
        zg[pl.ds(row, BLOCK), :] = dot(t, wgi[:, :COLS]) + dot(lifted, up_ref[:, :COLS])
        zi[pl.ds(row + 8, BLOCK), :] = dot(t, wgi[:, COLS:]) + dot(lifted, up_ref[:, COLS:])
        zb[pl.ds(row + 8, BLOCK), :] = dot(t, wbc[...])

    def project_all(blocks):
        for b in blocks:
            project(b)

    project_all([e])
    for k in (1, 2, 3, 4):
        landed(others[0], k)
    project_all([others[0]])
    take(bm, 1, 0, plus)
    take(bp, 3, 1, minus)
    take(bm, 2, 0, plus)
    take(bp, 4, 1, minus)
    for k, j in ((3, 1), (4, 2)):
        take(bm, k, 0)
        take(bp, j, 1)
    project_all([bm, bp])
    for b in others[1:3]:
        for k in (1, 2, 3, 4):
            landed(b, k)
    project_all(others[1:3])
    for k in (1, 3, 2, 4):
        take(bo, k, 2)
    project_all([bo])
    for k in (1, 2, 3, 4):
        landed(others[3], k)
    project_all([others[3]])

    def rim_copies():
        return [
            pltpu.make_async_remote_copy(
                src_ref=zi.at[pl.ds(ROWS, 8)], dst_ref=rimx, send_sem=rims.at[0], recv_sem=rimr.at[0],
                device_id={"seq": (s + 1) % N_SEQ},
            ),
            pltpu.make_async_remote_copy(
                src_ref=zb.at[pl.ds(ROWS, 8)], dst_ref=rimb, send_sem=rims.at[1], recv_sem=rimr.at[1],
                device_id={"seq": (s + 1) % N_SEQ},
            ),
        ]

    for copy in rim_copies():
        copy.start()

    sbias, rate = lane_row(sbias_ref, 1), lane_row(rate_ref, 1)
    direct = lane_row(direct_ref, 64)
    ri = lax.broadcasted_iota(jnp.int32, (BLOCK, BLOCK), 0)
    ci = lax.broadcasted_iota(jnp.int32, (BLOCK, BLOCK), 1)
    causal = ri >= ci
    left = ci < 64

    def conv(window, taps, bias):
        acc = bias
        for j in range(4):
            acc = acc + taps[j : j + 1, :] * window[5 + j : 5 + j + BLOCK, :]
        return silu(acc)

    def local(k, carry):
        state, offset = carry
        row = pl.multiple_of(k * BLOCK, BLOCK)
        xc = conv(zi[pl.ds(row, BLOCK + 8), :], taps_ref, bias_ref[...][None, :])
        bc = conv(zb[pl.ds(row, BLOCK + 8), :], btaps_ref, bbias_ref[...][None, :])
        raw = sd[pl.ds(row, BLOCK), :]
        raw = jnp.concatenate([raw, jnp.zeros((BLOCK, 128 - raw.shape[1]), F32)], 1) + sbias
        step = jnp.maximum(raw, 0.0) + jnp.log1p(jnp.exp(-jnp.abs(raw)))
        decay = -rate * step
        cum = lax.dot_general(
            causal.astype(F32), decay, NN, precision=lax.Precision.HIGHEST, preferred_element_type=F32
        )
        cum_t, step_t = cum.T, step.T
        bmap, cmap = bc[:, :STATE], bc[:, STATE:]
        b2, c2 = split(bmap), split(cmap)
        gram = dot3(c2, b2, NT)
        b_t = bmap.T
        inter = dot3(c2, split(state))
        cc[0, pl.ds(row, BLOCK), :] = c2[0]
        cc[1, pl.ds(row, BLOCK), :] = c2[1]
        ys, us, ecs, tots = [], [], [], []
        for p in range(3):
            ws, bs, cols, tot = [], [], [], []
            for h in (2 * p, 2 * p + 1):
                ch = jnp.broadcast_to(cum[:, h : h + 1], (BLOCK, BLOCK))
                rh = cum_t[h : h + 1, :]
                th = cum[BLOCK - 1 : BLOCK, h : h + 1]
                seg = jnp.exp(jnp.where(causal, ch - rh, -1e30))
                sh = step_t[h : h + 1, :]
                ws.append(gram * seg * sh)
                bs.append(b_t * (jnp.exp(th - rh) * sh))
                cols.append(ch)
                tot.append(jnp.broadcast_to(th, (1, 128)))
            lhs = jnp.concatenate([jnp.concatenate(ws, 1), jnp.concatenate(bs, 1)], 0)
            xp = xc[:, 128 * p : 128 * p + 128]
            rhs = jnp.concatenate([jnp.where(left, xp, 0.0), jnp.where(left, 0.0, xp)], 0)
            both = dot3(split(lhs), split(rhs))
            ecp = jnp.exp(jnp.where(left, cols[0], cols[1]))
            ys.append(both[:BLOCK] + ecp * inter[:, 128 * p : 128 * p + 128])
            us.append(both[BLOCK:])
            ecs.append(ecp)
            tots.append(jnp.exp(jnp.where(left[:1], tot[0], tot[1])))
        tot = jnp.concatenate(tots, 1)
        ybuf[pl.ds(row, BLOCK), :] = jnp.concatenate(ys, 1) + direct * xc
        ec[pl.ds(row, BLOCK), :] = jnp.concatenate(ecs, 1) * offset
        return tot * state + jnp.concatenate(us, 1), offset * tot

    for copy in rim_copies():
        copy.wait()
    started = s > 0
    zi[pl.ds(0, 8), :] = jnp.where(started, rimx[...], 0.0)
    zb[pl.ds(0, 8), :] = jnp.where(started, rimb[...], 0.0)

    state, total = lax.fori_loop(
        0, ROWS // BLOCK, local, (jnp.zeros((STATE, COLS), F32), jnp.ones((1, COLS), F32))
    )

    for j in range(N_SEQ):
        f1[j, pl.ds(0, 4), :] = state[4 * j : 4 * j + 4, :]
        f1[j, pl.ds(4, 1), :] = total

    def first(d):
        to = (s + d) % N_SEQ
        return pltpu.make_async_remote_copy(
            src_ref=f1.at[to], dst_ref=r1.at[s], send_sem=s1.at[d], recv_sem=v1.at[s], device_id={"seq": to}
        )

    def first_in(d):
        at = (s + d) % N_SEQ
        return pltpu.make_async_remote_copy(
            src_ref=f1.at[at], dst_ref=r1.at[at], send_sem=s1.at[d], recv_sem=v1.at[at], device_id={"seq": at}
        )

    @pl.loop(1, N_SEQ)
    def _(d):
        first(d).start()

    r1[s] = f1[s]

    @pl.loop(1, N_SEQ)
    def _(d):
        first_in(d).wait_recv()

    run = jnp.zeros((4, COLS), F32)
    for r in range(N_SEQ):
        o2[r] = run
        run = run * r1[r, pl.ds(4, 1), :] + r1[r, pl.ds(0, 4), :]

    def second(d):
        to = (s + d) % N_SEQ
        return pltpu.make_async_remote_copy(
            src_ref=o2.at[to], dst_ref=r2.at[s], send_sem=s2.at[d], recv_sem=v2.at[s], device_id={"seq": to}
        )

    def second_in(d):
        at = (s + d) % N_SEQ
        return pltpu.make_async_remote_copy(
            src_ref=o2.at[at], dst_ref=r2.at[at], send_sem=s2.at[d], recv_sem=v2.at[at], device_id={"seq": at}
        )

    @pl.loop(1, N_SEQ)
    def _(d):
        second(d).start()

    r2[s] = o2[s]

    @pl.loop(0, ROWS // BLOCK)
    def _(k):
        row = pl.multiple_of(k * BLOCK, BLOCK)
        zg[pl.ds(row, BLOCK), :] = silu(zg[pl.ds(row, BLOCK), :])

    @pl.loop(1, N_SEQ)
    def _(d):
        second_in(d).wait_recv()

    for j in range(N_SEQ):
        ebuf[pl.ds(4 * j, 4), :] = r2[j]
    entering = split(ebuf[...])
    ones = jnp.ones((8, COLS), BF16)

    @pl.loop(0, ROWS // BLOCK)
    def _(k):
        row = pl.multiple_of(k * BLOCK, BLOCK)
        at = pl.ds(row, BLOCK)
        far = dot3((cc[0, at, :], cc[1, at, :]), entering)
        gated = (ybuf[at, :] + ec[at, :] * far) * zg[at, :]
        ybuf[at, :] = gated
        qh, ql = split(gated * gated)
        sq[k] = (dot(ones, qh, NT) + dot(ones, ql, NT))[:1, :]

    def third(d):
        to = (e + d) % N_EXP
        return pltpu.make_async_remote_copy(
            src_ref=sq, dst_ref=r3.at[e], send_sem=s3.at[d], recv_sem=v3.at[e], device_id={"exp": to}
        )

    def third_in(d):
        at = (e + d) % N_EXP
        return pltpu.make_async_remote_copy(
            src_ref=sq, dst_ref=r3.at[at], send_sem=s3.at[d], recv_sem=v3.at[at], device_id={"exp": at}
        )

    for d in range(1, N_EXP):
        third(d).start()
    r3[e] = sq[...]
    for d in range(1, N_EXP):
        third_in(d).wait_recv()
    scl[...] = lax.rsqrt(jnp.sum(r3[...], axis=0) / INNER_WIDTH + 1e-05)
    gain = norm_ref[...][None, :]

    @pl.loop(0, ROWS // BLOCK)
    def _(k):
        at = pl.ds(pl.multiple_of(k * BLOCK, BLOCK), BLOCK)
        scale = jnp.broadcast_to(scl[k], (BLOCK, 128)).T
        scale = jnp.concatenate([scale] * 3, 1)
        out_ref[at, :] = (ybuf[at, :] * scale * gain).astype(BF16)

    for copy in sent:
        copy.wait_send()

    @pl.loop(1, N_SEQ)
    def _(d):
        first(d).wait_send()
        second(d).wait_send()

    for d in range(1, N_EXP):
        third(d).wait_send()


def body(
    tokens, routes, gate_inner_weight, state_map_weight, step_size_weight, adapter_down_weight,
    adapter_up_weight, inner_conv_taps, state_map_taps, inner_conv_bias, state_map_conv_bias,
    step_size_bias, head_decay_rate, direct_head_scale, gated_norm_scale,
):
    vmem, smem, anyw = (
        pl.BlockSpec(memory_space=pltpu.VMEM),
        pl.BlockSpec(memory_space=pltpu.SMEM),
        pl.BlockSpec(memory_space=pl.ANY),
    )
    dma = pltpu.SemaphoreType.DMA
    return pl.pallas_call(
        kernel,
        out_shape=jax.ShapeDtypeStruct((ROWS, COLS), BF16),
        in_specs=[anyw, vmem, anyw, anyw, vmem, anyw, vmem] + [vmem] * 4 + [smem] * 3 + [vmem],
        out_specs=vmem,
        scratch_shapes=[
            pltpu.VMEM((N_EXP, SEG, MODEL), BF16),
            pltpu.VMEM((N_EXP, 1, 128), jnp.int32),
            pltpu.VMEM((MODEL, 2 * COLS), BF16),
            pltpu.VMEM((MODEL, 2 * STATE), BF16),
            pltpu.VMEM((SEG, MODEL), BF16),
            pltpu.VMEM((ROWS, COLS), F32),
            pltpu.VMEM((ROWS + 8, COLS), F32),
            pltpu.VMEM((ROWS + 8, 2 * STATE), F32),
            pltpu.VMEM((ROWS, 16), F32),
            pltpu.VMEM((8, COLS), F32),
            pltpu.VMEM((8, 2 * STATE), F32),
            pltpu.VMEM((2, ROWS, STATE), BF16),
            pltpu.VMEM((ROWS, COLS), F32),
            pltpu.VMEM((ROWS, COLS), F32),
            pltpu.VMEM((N_SEQ, 5, COLS), F32),
            pltpu.VMEM((N_SEQ, 5, COLS), F32),
            pltpu.VMEM((N_SEQ, 4, COLS), F32),
            pltpu.VMEM((N_SEQ, 4, COLS), F32),
            pltpu.VMEM((STATE, COLS), F32),
            pltpu.VMEM((8, 1, 128), F32),
            pltpu.VMEM((N_EXP, 8, 1, 128), F32),
            pltpu.VMEM((8, 1, 128), F32),
            dma((4,)),
            dma((N_EXP, 5)),
            dma((3, 5)),
            dma((5,)),
            dma((3, 5)),
            dma((N_EXP,)),
            dma((N_EXP,)),
            dma((2,)),
            dma((2,)),
            dma((N_SEQ,)),
            dma((N_SEQ,)),
            dma((N_SEQ,)),
            dma((N_SEQ,)),
            dma((N_EXP,)),
            dma((N_EXP,)),
        ],
        compiler_params=pltpu.CompilerParams(
            collective_id=0, has_side_effects=True, vmem_limit_bytes=62 * 1024 * 1024
        ),
    )(
        tokens, routes.T, gate_inner_weight.reshape(MODEL, 2 * COLS), state_map_weight,
        step_size_weight.T, adapter_down_weight.T, adapter_up_weight.reshape(128, 2 * COLS),
        inner_conv_taps, state_map_taps, inner_conv_bias, state_map_conv_bias,
        step_size_bias, head_decay_rate, direct_head_scale, gated_norm_scale,
    )


def solution(mesh):
    both = ("seq", "exp")
    in_specs = (
        P(both, None),
        P(both, None),
        P(None, None, "exp"),
        P(),
        P(None, "exp"),
        P(None, "exp"),
        P(None, None, "exp"),
        P(None, "exp"),
        P(),
        P("exp"),
        P(),
        P("exp"),
        P("exp"),
        P("exp"),
        P("exp"),
    )
    return jax.shard_map(
        body, mesh=mesh, in_specs=in_specs, out_specs=P("seq", "exp"), check_vma=False
    )
```

time: 260 us -> 102 us (0.39)
  Pallas kernels: 0 us -> 93.1 us
  local copies, waits for them, and re-layouts: 69.9 us -> 8.38 us
  blocking collectives: 56.9 us -> 0 us
  matrix products: 43.5 us -> 0 us
  waiting for transfers between devices: 40.2 us -> 0 us
  other arithmetic: 20.2 us -> 0 us
  between operations: 14.4 us -> 0.01 us
  starting transfers between devices: 13 us -> 0 us
    pallas_call x0 -> x1, Pallas kernels: none -> 93.1 us  [body(): pl.pallas_call(kernel, out_shape=jax.ShapeDtypeStruct((ROWS, COLS), BF16)...]
    dynamic_update_slice x8 -> x0, local copies, waits for them, and re-layouts: 39.7 us -> none  [run_blocks(): final, output = lax.scan(block_step, state, items)]
    all_gather x2 -> x0, waiting for transfers between devices: 39.4 us -> none  [the longest x1 19.9 us: entering_2(): pieces = jax.tree.map(lambda part: lax.all_gather(part, axis), running)]
    dot_general x17 -> x0, matrix products: 36.6 us -> none  [the longest x1 9.51 us: body(): jnp.dot(whole, gate_inner_weight.reshape(features, 2 * split_widths), pre...]
    all_gather x3 -> x0, blocking collectives: 34.9 us -> none  [the longest x2 23.9 us: entering_2(): pieces = jax.tree.map(lambda part: lax.all_gather(part, axis), running)]
    all_to_all x1 -> x0, blocking collectives: 13.3 us -> none  [copy_for_each(): lax.all_to_all(jnp.broadcast_to(value[None], (size, *value.shape)), axis,...]
    another operation x10 -> x0, other arithmetic: 9.32 us -> none
    unnamed x1 -> x0, blocking collectives: 8.62 us -> none
  transfers between devices with their start and end apart: 5 -> 0, of which waited for: 2 -> 0; matrix products, arithmetic and copies ran while one was open for 10% -> 0% of each run, Pallas kernels for 0% -> 0%
where the time goes in v1:
time: 102 us; the launch traced here: 101 us
  Pallas kernels  93.1 us (91%)
  local copies, waits for them, and re-layouts  8.38 us (8%)
    pallas_call x1, Pallas kernels, body(): pl.pallas_call(kernel, out_shape=jax.ShapeDtypeStruct((ROWS, COLS), BF16)...  93.1 us
    unnamed x3, local copies, waits for them, and re-layouts  8.38 us

profile of v1, /device:TPU:1, one launch (start us, length us, event | category | flops | bytes accessed | tf_op | source)
XLA Modules:
  0.0 101.5 jit_solution(18018105827512343190)
XLA Ops:
  0.0 1.6 %copy.17 = bf16[16,8,2,384]{3,1,2,0:T(8,128)(2,1)} copy(bf16[16,8,2,384]{3,2,1,0:T(2,128)(2,1)} %bitcast.10) | data formatting | bytes 393216
  1.6 4.7 %copy.16 = bf16[320,8,2,384]{3,1,2,0:T(8,128)(2,1)} copy(bf16[320,8,2,384]{3,2,1,0:T(2,128)(2,1)} %bitcast.8) | data formatting | bytes 7864320
  6.3 93.1 %shard_map.145 = bf16[1024,384]{1,0:T(8,128)(2,1)} custom-call(bf16[128,2560]{1,0:T(8,128)(2,1)} %tok_hbm.1, s32[1,128]{1,0:T(1,128)} %bitcast.13, bf16[2560,768]{1,0:T(8,128)(2,1)} %bitcast.7, bf16[2560,256]{1,0:T(8,128)(2,1)} %wbc_hbm.1, bf16[6,2560]{1,0:T(8,128)(2,1)} %bitcast.12, bf16[16,2560]{1,0:T(8,128)(2,1)} %bitcast.11, bf16[128,768]{1,0:T(8,128)(2,1)} %bitcast.9, ...), custom_call_target="tpu_custom_call" | custom-call | tf_op jit(solution)/shard_map/pallas_call | solution.py:393
  99.4 2.1 %copy.19 = bf16[1024,384]{1,0:T(8,128)(2,1)} copy(bf16[1024,384]{1,0:T(8,128)(2,1)} %shard_map.145) | data formatting | bytes 1572864

commit v2 on v1

v2 whole, which is shorter than its diff:
```python
import functools

import jax
import jax.numpy as jnp
from jax import lax
from jax.experimental import pallas as pl
from jax.experimental.pallas import tpu as pltpu
from jax.sharding import PartitionSpec as P

MODEL = 2560
STATE = 128
HEADS = 6
COLS = 384
RANK = 8
BLOCK = 128
N_EXP = 8
N_SEQ = 32
ROWS = 1024
INNER_WIDTH = 3072
SEG = 144
PIECES = ((128, 16), (0, 32), (32, 32), (64, 32), (96, 32))
F32, BF16 = jnp.float32, jnp.bfloat16
NT = (((1,), (1,)), ((), ()))
NN = (((1,), (0,)), ((), ()))


def dot(a, b, dims=NN):
    return lax.dot_general(a, b, dims, preferred_element_type=F32)


def split(a):
    hi = a.astype(BF16)
    return hi, (a - hi.astype(F32)).astype(BF16)


def dot3(a, b, dims=NN):
    (ah, al), (bh, bl) = a, b
    return dot(ah, bh, dims) + (dot(ah, bl, dims) + dot(al, bh, dims))


def silu(v):
    return v / (1.0 + jnp.exp(-v))


def lane_row(ref, width):
    lane = lax.broadcasted_iota(jnp.int32, (1, 128 if width == 1 else HEADS * width), 1) // width
    row = jnp.zeros(lane.shape, F32)
    for h in range(HEADS):
        row = jnp.where(lane == h, ref[h], row)
    return row


def kernel(
    tok_hbm, routes_hbm, wgi_hbm, wbc_hbm, dt_hbm, down_hbm, up3_hbm,
    taps_hbm, btaps_hbm, bias_hbm, bbias_hbm, sbias_ref, rate_ref, direct_ref, norm_hbm,
    out_ref,
    routes_ref, dt_ref, up3_ref, taps_ref, btaps_ref, bias_ref, bbias_ref, norm_ref, tall, routes, wraw, wgi, wbc, ddt, up, zg, zi, zb, sd, rimx, rimb,
    cc, ybuf, ec, xcb, bsp, cumb, cumt, stept, uu, tots, f1, r1, o2, r2, ebuf, sq, r3,
    lsem, rsem, ssem, fsem, csem, rtr, rts, rimr, rims, s1, v1, s2, v2, s3, v3,
):
    e, s = lax.axis_index("exp"), lax.axis_index("seq")
    y, c = e // 2, e % 2
    yp, ym, yo = (y + 1) % 4, (y + 3) % 4, (y + 2) % 4
    plus, minus, mate = yp * 2 + c, ym * 2 + c, y * 2 + 1 - c

    loads = [
        pltpu.make_async_copy(tok_hbm, tall.at[e, pl.ds(0, 128)], lsem.at[0]),
        pltpu.make_async_copy(down_hbm, tall.at[e, pl.ds(128, 16)], lsem.at[1]),
        pltpu.make_async_copy(wgi_hbm, wraw, lsem.at[2]),
        pltpu.make_async_copy(wbc_hbm, wbc, lsem.at[3]),
        pltpu.make_async_copy(routes_hbm, routes_ref, lsem.at[4]),
        pltpu.make_async_copy(dt_hbm, dt_ref, lsem.at[5]),
        pltpu.make_async_copy(up3_hbm, up3_ref, lsem.at[6]),
        pltpu.make_async_copy(taps_hbm, taps_ref, lsem.at[7]),
        pltpu.make_async_copy(btaps_hbm, btaps_ref, lsem.at[8]),
        pltpu.make_async_copy(bias_hbm, bias_ref, lsem.at[9]),
        pltpu.make_async_copy(bbias_hbm, bbias_ref, lsem.at[10]),
        pltpu.make_async_copy(norm_hbm, norm_ref, lsem.at[11]),
    ]
    for load in loads:
        load.start()

    barrier = pltpu.get_barrier_semaphore()
    for d in range(1, N_EXP):
        pl.semaphore_signal(barrier, inc=1, device_id={"exp": (e + d) % N_EXP})

    @pl.loop(1, N_SEQ)
    def _(d):
        pl.semaphore_signal(barrier, inc=1, device_id={"seq": (s + d) % N_SEQ})

    ddt[...] = jnp.zeros_like(ddt)
    for i in (0, 1, 4, 5, 6, 7, 8, 9, 10, 11):
        loads[i].wait()
    routes[e] = routes_ref[...]
    ddt[pl.ds(128, HEADS), :] = dt_ref[...]
    pl.semaphore_wait(barrier, N_EXP - 1 + N_SEQ - 1)

    def piece(b, k):
        first, size = PIECES[k]
        return tall.at[b, pl.ds(first, size)]

    def push(b, k, to, sem):
        copy = pltpu.make_async_remote_copy(
            src_ref=piece(b, k), dst_ref=piece(b, k), send_sem=sem, recv_sem=rsem.at[b, k],
            device_id={"exp": to},
        )
        copy.start()
        sent.append(copy)

    def landed(b, k):
        pltpu.make_async_remote_copy(
            src_ref=piece(b, k), dst_ref=piece(b, k), send_sem=lsem.at[0], recv_sem=rsem.at[b, k],
            device_id={"exp": mate},
        ).wait_recv()

    sent = []
    for d in range(1, N_EXP):
        copy = pltpu.make_async_remote_copy(
            src_ref=routes_ref, dst_ref=routes.at[e], send_sem=rts.at[d], recv_sem=rtr.at[e],
            device_id={"exp": (e + d) % N_EXP},
        )
        copy.start()
        sent.append(copy)
    for k in range(5):
        push(e, k, mate, ssem.at[2, k])
    push(e, 0, plus, ssem.at[0, 0])
    push(e, 0, minus, ssem.at[1, 0])
    push(e, 1, plus, ssem.at[0, 1])
    push(e, 3, minus, ssem.at[1, 3])

    def take(b, k, slot, forward=None):
        landed(b, k)
        if forward is not None:
            push(b, k, forward, fsem.at[k])
        push(b, k, mate, csem.at[slot, k])

    bm, bp, bo = ym * 2 + c, yp * 2 + c, yo * 2 + c
    others = [y * 2 + 1 - c, ym * 2 + 1 - c, yp * 2 + 1 - c, yo * 2 + 1 - c]

    loads[2].wait()
    loads[3].wait()

    @pl.loop(0, MODEL // 32)
    def _(i):
        at = pl.ds(pl.multiple_of(i * 32, 32), 32)
        wgi[at, :] = wraw[at, :, :].reshape(32, 2 * COLS)

    up[...] = up3_ref[...].reshape(128, 2 * COLS)

    expert_of_lane = lax.broadcasted_iota(jnp.int32, (BLOCK, 128), 1) // RANK

    def main(b):
        t = tall[b, pl.ds(0, BLOCK), :]
        row = pl.multiple_of(b * BLOCK, BLOCK)
        zg[pl.ds(row, BLOCK), :] = dot(t, wgi[:, :COLS])
        zi[pl.ds(row + 8, BLOCK), :] = dot(t, wgi[:, COLS:])
        zb[pl.ds(row + 8, BLOCK), :] = dot(t, wbc[...])

    def routed(b):
        t = tall[b, pl.ds(0, BLOCK), :]
        row = pl.multiple_of(b * BLOCK, BLOCK)
        aux = dot(t, ddt[...], NT)
        sd[pl.ds(row, BLOCK), :] = aux[:, 128:]
        route = jnp.broadcast_to(routes[b].astype(F32), (BLOCK, 128)).T.astype(jnp.int32)
        lifted = jnp.where(route == expert_of_lane, aux[:, :128], 0.0).astype(BF16)
        zg[pl.ds(row, BLOCK), :] += dot(lifted, up[:, :COLS])
        zi[pl.ds(row + 8, BLOCK), :] += dot(lifted, up[:, COLS:])

    take(bm, 0, 0, plus)
    for k in (2, 3, 4):
        push(e, k, plus, ssem.at[0, k])
    for k in (4, 1, 2):
        push(e, k, minus, ssem.at[1, k])
    take(bp, 0, 1)
    main(e)
    for k in (1, 2, 3, 4):
        landed(others[0], k)
    main(others[0])
    take(bm, 1, 0, plus)
    take(bp, 3, 1, minus)
    take(bo, 0, 2)
    for b in others:
        landed(b, 0)
    for d in range(1, N_EXP):
        b = (e + d) % N_EXP
        pltpu.make_async_remote_copy(
            src_ref=routes_ref, dst_ref=routes.at[b], send_sem=lsem.at[0], recv_sem=rtr.at[b],
            device_id={"exp": mate},
        ).wait_recv()
    for b in range(N_EXP):
        ddt[pl.ds(16 * b, 16), :] = tall[b, pl.ds(128, 16), :]
    routed(e)
    routed(others[0])
    take(bp, 4, 1, minus)
    take(bm, 2, 0, plus)

    sbias, rate = lane_row(sbias_ref, 1), lane_row(rate_ref, 1)
    direct = lane_row(direct_ref, 64)
    ri = lax.broadcasted_iota(jnp.int32, (BLOCK, BLOCK), 0)
    ci = lax.broadcasted_iota(jnp.int32, (BLOCK, BLOCK), 1)
    causal = ri >= ci
    lower = causal.astype(F32)
    left = ci < 64

    def conv(window, taps, bias):
        acc = bias
        for j in range(4):
            acc = acc + taps[j : j + 1, :] * window[5 + j : 5 + j + BLOCK, :]
        return silu(acc)

    def side_by_side(xp):
        return split(jnp.concatenate([jnp.where(left, xp, 0.0), jnp.where(left, 0.0, xp)], 0))

    def states(k):
        row = pl.multiple_of(k * BLOCK, BLOCK)
        at = pl.ds(row, BLOCK)
        xc = conv(zi[pl.ds(row, BLOCK + 8), :], taps_ref, bias_ref[...][None, :])
        bmap = conv(zb[pl.ds(row, BLOCK + 8), :STATE], btaps_ref[:, :STATE], bbias_ref[...][None, :STATE])
        raw = sd[at, :]
        raw = jnp.concatenate([raw, jnp.zeros((BLOCK, 128 - raw.shape[1]), F32)], 1) + sbias
        step = jnp.maximum(raw, 0.0) + jnp.log1p(jnp.exp(-jnp.abs(raw)))
        decay = -rate * step
        cum = lax.dot_general(
            lower, decay, NN, precision=lax.Precision.HIGHEST, preferred_element_type=F32
        )
        cum_t, step_t = cum.T[:8], step.T[:8]
        xcb[at, :] = xc
        bh, bl = split(bmap)
        bsp[0, at, :] = bh
        bsp[1, at, :] = bl
        cumb[at, :] = cum
        cumt[k] = cum_t
        stept[k] = step_t
        b_t = bmap.T
        us, ts = [], []
        for p in range(3):
            bs, tot = [], []
            for h in (2 * p, 2 * p + 1):
                th = cum[BLOCK - 1 : BLOCK, h : h + 1]
                bs.append(b_t * (jnp.exp(th - cum_t[h : h + 1, :]) * step_t[h : h + 1, :]))
                tot.append(jnp.broadcast_to(th, (1, 128)))
            us.append(dot3(split(jnp.concatenate(bs, 1)), side_by_side(xc[:, 128 * p : 128 * p + 128])))
            ts.append(jnp.exp(jnp.where(left[:1], tot[0], tot[1])))
        uu[k] = jnp.concatenate(us, 1)
        tots[k] = jnp.concatenate(ts, 1)

    def states_but_first(k):
        @pl.when(k != 0)
        def _():
            states(k)

    states_but_first(2 * y + 1)
    for k in (1, 2):
        take(bp, k, 1)
    main(bp)
    routed(bp)
    for k in (1, 2, 3, 4):
        landed(others[2], k)
    main(others[2])
    routed(others[2])
    for k in (3, 4):
        take(bm, k, 0)
    main(bm)
    routed(bm)
    for k in (1, 2, 3, 4):
        landed(others[1], k)
    main(others[1])
    routed(others[1])
    states_but_first(2 * yp)
    take(bo, 3, 2)
    states_but_first(2 * yp + 1)
    take(bo, 1, 2)
    states_but_first(2 * y)
    states_but_first(2 * ym + 1)
    for k in (4, 2):
        take(bo, k, 2)
    main(bo)
    routed(bo)
    for k in (1, 2, 3, 4):
        landed(others[3], k)
    main(others[3])
    routed(others[3])

    def rim_copies():
        return [
            pltpu.make_async_remote_copy(
                src_ref=zi.at[pl.ds(ROWS, 8)], dst_ref=rimx, send_sem=rims.at[0], recv_sem=rimr.at[0],
                device_id={"seq": (s + 1) % N_SEQ},
            ),
            pltpu.make_async_remote_copy(
                src_ref=zb.at[pl.ds(ROWS, 8)], dst_ref=rimb, send_sem=rims.at[1], recv_sem=rimr.at[1],
                device_id={"seq": (s + 1) % N_SEQ},
            ),
        ]

    for copy in rim_copies():
        copy.start()

    states_but_first(2 * yo)
    states_but_first(2 * yo + 1)
    states_but_first(2 * ym)
    for copy in rim_copies():
        copy.wait()
    started = s > 0
    zi[pl.ds(0, 8), :] = jnp.where(started, rimx[...], 0.0)
    zb[pl.ds(0, 8), :] = jnp.where(started, rimb[...], 0.0)
    states(0)

    state, total = jnp.zeros((STATE, COLS), F32), jnp.ones((1, COLS), F32)
    for k in range(ROWS // BLOCK):
        update, tot = uu[k], tots[k]
        uu[k] = state
        tots[k] = total
        state, total = tot * state + update, total * tot

    spare = jnp.concatenate([total[:, 128 * p : 128 * p + 128] for p in (0, 1, 2, 2)], 0)
    for j in range(N_SEQ):
        f1[j] = jnp.concatenate([state[4 * j : 4 * j + 4, :], spare], 1)

    x, z = s % 4, s // 4
    offsets = sorted(
        ((i, j) for i in range(8) for j in range(4) if i or j),
        key=lambda o: -min(o[0], 8 - o[0]) - min(o[1], 4 - o[1]),
    )

    def away(d):
        i, j = offsets[d - 1]
        return (z + i) % 8 * 4 + (x + j) % 4

    def first(d):
        to = away(d)
        return pltpu.make_async_remote_copy(
            src_ref=f1.at[to], dst_ref=r1.at[s], send_sem=s1.at[d], recv_sem=v1.at[s], device_id={"seq": to}
        )

    def first_in(d):
        at = (s + d) % N_SEQ
        return pltpu.make_async_remote_copy(
            src_ref=f1.at[at], dst_ref=r1.at[at], send_sem=s1.at[d], recv_sem=v1.at[at], device_id={"seq": at}
        )

    for d in range(1, N_SEQ):
        first(d).start()

    r1[s] = f1[s]

    @pl.loop(0, ROWS // BLOCK)
    def _(k):
        row = pl.multiple_of(k * BLOCK, BLOCK)
        at = pl.ds(row, BLOCK)
        cmap = conv(zb[pl.ds(row, BLOCK + 8), STATE:], btaps_ref[:, STATE:], bbias_ref[...][None, STATE:])
        c2 = split(cmap)
        cc[0, at, :], cc[1, at, :] = c2
        gram = dot3(c2, (bsp[0, at, :], bsp[1, at, :]), NT)
        inter = dot3(c2, split(uu[k]))
        cum, cum_t, step_t, xc = cumb[at, :], cumt[k], stept[k], xcb[at, :]
        ys, ecs = [], []
        for p in range(3):
            ws, cols = [], []
            for h in (2 * p, 2 * p + 1):
                ch = jnp.broadcast_to(cum[:, h : h + 1], (BLOCK, BLOCK))
                seg = jnp.exp(jnp.where(causal, ch - cum_t[h : h + 1, :], -1e30))
                ws.append(gram * seg * step_t[h : h + 1, :])
                cols.append(ch)
            near = dot3(split(jnp.concatenate(ws, 1)), side_by_side(xc[:, 128 * p : 128 * p + 128]))
            ecp = jnp.exp(jnp.where(left, cols[0], cols[1]))
            ys.append(near + ecp * inter[:, 128 * p : 128 * p + 128])
            ecs.append(ecp)
        ybuf[at, :] = jnp.concatenate(ys, 1) + direct * xc
        ec[at, :] = jnp.concatenate(ecs, 1) * tots[k]

    @pl.loop(1, N_SEQ)
    def _(d):
        first_in(d).wait_recv()

    run = [jnp.zeros((4, 128), F32)] * 3
    for r in range(N_SEQ):
        o2[r] = jnp.concatenate(run, 1)
        come = r1[r]
        run = [
            run[p] * come[p : p + 1, COLS:] + come[:, 128 * p : 128 * p + 128] for p in range(3)
        ]

    def second(d):
        to = away(d)
        return pltpu.make_async_remote_copy(
            src_ref=o2.at[to], dst_ref=r2.at[s], send_sem=s2.at[d], recv_sem=v2.at[s], device_id={"seq": to}
        )

    def second_in(d):
        at = (s + d) % N_SEQ
        return pltpu.make_async_remote_copy(
            src_ref=o2.at[at], dst_ref=r2.at[at], send_sem=s2.at[d], recv_sem=v2.at[at], device_id={"seq": at}
        )

    for d in range(1, N_SEQ):
        second(d).start()

    r2[s] = o2[s]

    @pl.loop(0, ROWS // BLOCK)
    def _(k):
        row = pl.multiple_of(k * BLOCK, BLOCK)
        zg[pl.ds(row, BLOCK), :] = silu(zg[pl.ds(row, BLOCK), :])

    @pl.loop(1, N_SEQ)
    def _(d):
        second_in(d).wait_recv()

    for j in range(N_SEQ):
        ebuf[pl.ds(4 * j, 4), :] = r2[j]
    entering = split(ebuf[...])

    def third(half, d):
        to = (e + d) % N_EXP
        return pltpu.make_async_remote_copy(
            src_ref=sq.at[half], dst_ref=r3.at[half, e], send_sem=s3.at[half, d],
            recv_sem=v3.at[half, e], device_id={"exp": to},
        )

    def third_in(half, d):
        at = (e + d) % N_EXP
        return pltpu.make_async_remote_copy(
            src_ref=sq.at[half], dst_ref=r3.at[half, at], send_sem=s3.at[half, d],
            recv_sem=v3.at[half, at], device_id={"exp": at},
        )

    for half in (0, 1):
        for k in (0, 2):
            at = pl.ds(512 * half + 128 * k, 2 * BLOCK)
            far = dot3((cc[0, at, :], cc[1, at, :]), entering)
            gated = (ybuf[at, :] + ec[at, :] * far) * zg[at, :]
            ybuf[at, :] = gated
            gated = gated * gated
            gated = gated[:, :128] + gated[:, 128:256] + gated[:, 256:]
            for i in (0, 1):
                sq[half, k + i] = jnp.sum(gated[128 * i : 128 * i + 128].T, axis=0, keepdims=True)
        for d in range(1, N_EXP):
            third(half, d).start()
    gain = norm_ref[...][None, :]
    for half in (0, 1):
        r3[half, e] = sq[half]
        for d in range(1, N_EXP):
            third_in(half, d).wait_recv()
        scale = lax.rsqrt(jnp.sum(r3[half], axis=0) / INNER_WIDTH + 1e-05)
        for k in range(4):
            at = pl.ds(512 * half + 128 * k, BLOCK)
            wide = jnp.broadcast_to(scale[k], (BLOCK, 128)).T
            wide = jnp.concatenate([wide] * 3, 1)
            out_ref[at, :] = (ybuf[at, :] * wide * gain).astype(BF16)

    for copy in sent:
        copy.wait_send()

    for d in range(1, N_SEQ):
        first(d).wait_send()
        second(d).wait_send()

    for half in (0, 1):
        for d in range(1, N_EXP):
            third(half, d).wait_send()


def body(
    tokens, routes, gate_inner_weight, state_map_weight, step_size_weight, adapter_down_weight,
    adapter_up_weight, inner_conv_taps, state_map_taps, inner_conv_bias, state_map_conv_bias,
    step_size_bias, head_decay_rate, direct_head_scale, gated_norm_scale,
):
    vmem, smem, hbm = (
        pl.BlockSpec(memory_space=pltpu.VMEM),
        pl.BlockSpec(memory_space=pltpu.SMEM),
        pl.BlockSpec(memory_space=pltpu.HBM),
    )
    dma = pltpu.SemaphoreType.DMA
    return pl.pallas_call(
        kernel,
        out_shape=jax.ShapeDtypeStruct((ROWS, COLS), BF16),
        in_specs=[hbm] * 11 + [smem] * 3 + [hbm],
        out_specs=vmem,
        scratch_shapes=[
            pltpu.VMEM((1, 128), jnp.int32),
            pltpu.VMEM((HEADS, MODEL), BF16),
            pltpu.VMEM((128, 2, COLS), BF16),
            pltpu.VMEM((4, COLS), F32),
            pltpu.VMEM((4, 2 * STATE), F32),
            pltpu.VMEM((COLS,), F32),
            pltpu.VMEM((2 * STATE,), F32),
            pltpu.VMEM((COLS,), F32),
            pltpu.VMEM((N_EXP, SEG, MODEL), BF16),
            pltpu.VMEM((N_EXP, 1, 128), jnp.int32),
            pltpu.VMEM((MODEL, 2, COLS), BF16),
            pltpu.VMEM((MODEL, 2 * COLS), BF16),
            pltpu.VMEM((MODEL, 2 * STATE), BF16),
            pltpu.VMEM((SEG, MODEL), BF16),
            pltpu.VMEM((128, 2 * COLS), BF16),
            pltpu.VMEM((ROWS, COLS), F32),
            pltpu.VMEM((ROWS + 8, COLS), F32),
            pltpu.VMEM((ROWS + 8, 2 * STATE), F32),
            pltpu.VMEM((ROWS, 16), F32),
            pltpu.VMEM((8, COLS), F32),
            pltpu.VMEM((8, 2 * STATE), F32),
            pltpu.VMEM((2, ROWS, STATE), BF16),
            pltpu.VMEM((ROWS, COLS), F32),
            pltpu.VMEM((ROWS, COLS), F32),
            pltpu.VMEM((ROWS, COLS), F32),
            pltpu.VMEM((2, ROWS, STATE), BF16),
            pltpu.VMEM((ROWS, 128), F32),
            pltpu.VMEM((8, 8, 128), F32),
            pltpu.VMEM((8, 8, 128), F32),
            pltpu.VMEM((8, STATE, COLS), F32),
            pltpu.VMEM((8, 1, COLS), F32),
            pltpu.VMEM((N_SEQ, 4, COLS + 128), F32),
            pltpu.VMEM((N_SEQ, 4, COLS + 128), F32),
            pltpu.VMEM((N_SEQ, 4, COLS), F32),
            pltpu.VMEM((N_SEQ, 4, COLS), F32),
            pltpu.VMEM((STATE, COLS), F32),
            pltpu.VMEM((2, 4, 1, 128), F32),
            pltpu.VMEM((2, N_EXP, 4, 1, 128), F32),
            dma((12,)),
            dma((N_EXP, 5)),
            dma((3, 5)),
            dma((5,)),
            dma((3, 5)),
            dma((N_EXP,)),
            dma((N_EXP,)),
            dma((2,)),
            dma((2,)),
            dma((N_SEQ,)),
            dma((N_SEQ,)),
            dma((N_SEQ,)),
            dma((N_SEQ,)),
            dma((2, N_EXP)),
            dma((2, N_EXP)),
        ],
        compiler_params=pltpu.CompilerParams(
            collective_id=0, has_side_effects=True, vmem_limit_bytes=62 * 1024 * 1024
        ),
    )(
        tokens, routes.T, gate_inner_weight, state_map_weight,
        step_size_weight.T, adapter_down_weight.T, adapter_up_weight,
        inner_conv_taps, state_map_taps, inner_conv_bias, state_map_conv_bias,
        step_size_bias, head_decay_rate, direct_head_scale, gated_norm_scale,
    )


def solution(mesh):
    both = ("seq", "exp")
    in_specs = (
        P(both, None),
        P(both, None),
        P(None, None, "exp"),
        P(),
        P(None, "exp"),
        P(None, "exp"),
        P(None, None, "exp"),
        P(None, "exp"),
        P(),
        P("exp"),
        P(),
        P("exp"),
        P("exp"),
        P("exp"),
        P("exp"),
    )
    return jax.shard_map(
        body, mesh=mesh, in_specs=in_specs, out_specs=P("seq", "exp"), check_vma=False
    )
```

time: 102 us -> 72.9 us (0.71)
  Pallas kernels: 93.1 us -> 70.7 us
  local copies, waits for them, and re-layouts: 8.38 us -> 2.09 us
    pallas_call x1, Pallas kernels: 93.1 us -> 70.7 us  [body(): pl.pallas_call(kernel, out_shape=jax.ShapeDtypeStruct((ROWS, COLS), BF16)...]
    unnamed x3 -> x1, local copies, waits for them, and re-layouts: 8.38 us -> 2.09 us
where the time goes in v2:
time: 72.9 us; the launch traced here: 72.8 us
  Pallas kernels  70.7 us (97%)
  local copies, waits for them, and re-layouts  2.09 us (3%)
    pallas_call x1, Pallas kernels, body(): pl.pallas_call(kernel, out_shape=jax.ShapeDtypeStruct((ROWS, COLS), BF16)...  70.7 us
    unnamed x1, local copies, waits for them, and re-layouts  2.09 us

profile of v2, /device:TPU:1, one launch (start us, length us, event | category | flops | bytes accessed | tf_op | source)
XLA Modules:
  0.0 72.8 jit_solution(2488355277357795951)
XLA Ops:
  0.0 70.7 %shard_map.145 = bf16[1024,384]{1,0:T(8,128)(2,1)} custom-call(bf16[128,2560]{1,0:T(8,128)(2,1)} %tok_hbm.1, s32[1,128]{1,0:T(1,128)} %bitcast.5, bf16[2560,2,384]{2,1,0:T(2,128)(2,1)} %wgi_hbm.1, bf16[2560,256]{1,0:T(8,128)(2,1)} %wbc_hbm.1, bf16[6,2560]{1,0:T(8,128)(2,1)} %bitcast.4, bf16[16,2560]{1,0:T(8,128)(2,1)} %bitcast.3, ...), custom_call_target="tpu_custom_call" | custom-call | tf_op jit(solution)/shard_map/pallas_call | solution.py:475
  70.7 2.1 %copy.17 = bf16[1024,384]{1,0:T(8,128)(2,1)} copy(bf16[1024,384]{1,0:T(8,128)(2,1)} %shard_map.145) | data formatting | bytes 1572864

commit v3 on v2

--- a/solution.py
+++ b/solution.py
@@ -199,7 +199,7 @@
     ri = lax.broadcasted_iota(jnp.int32, (BLOCK, BLOCK), 0)
     ci = lax.broadcasted_iota(jnp.int32, (BLOCK, BLOCK), 1)
     causal = ri >= ci
-    lower = causal.astype(F32)
+    lower = causal.astype(F32).astype(BF16)
     left = ci < 64
 
     def conv(window, taps, bias):
@@ -220,9 +220,9 @@
         raw = jnp.concatenate([raw, jnp.zeros((BLOCK, 128 - raw.shape[1]), F32)], 1) + sbias
         step = jnp.maximum(raw, 0.0) + jnp.log1p(jnp.exp(-jnp.abs(raw)))
         decay = -rate * step
-        cum = lax.dot_general(
-            lower, decay, NN, precision=lax.Precision.HIGHEST, preferred_element_type=F32
-        )
+        d1, rest = split(decay)[0], decay - split(decay)[0].astype(F32)
+        d2, d3 = split(rest)
+        cum = dot(lower, d1) + (dot(lower, d2) + dot(lower, d3))
         cum_t, step_t = cum.T[:8], step.T[:8]
         xcb[at, :] = xc
         bh, bl = split(bmap)
@@ -344,8 +344,7 @@
 
     r1[s] = f1[s]
 
-    @pl.loop(0, ROWS // BLOCK)
-    def _(k):
+    def inside(k):
         row = pl.multiple_of(k * BLOCK, BLOCK)
         at = pl.ds(row, BLOCK)
         cmap = conv(zb[pl.ds(row, BLOCK + 8), STATE:], btaps_ref[:, STATE:], bbias_ref[...][None, STATE:])
@@ -369,13 +368,17 @@
         ybuf[at, :] = jnp.concatenate(ys, 1) + direct * xc
         ec[at, :] = jnp.concatenate(ecs, 1) * tots[k]
 
+    @pl.loop(0, 6)
+    def _(k):
+        inside(k)
+
     @pl.loop(1, N_SEQ)
     def _(d):
         first_in(d).wait_recv()
 
     run = [jnp.zeros((4, 128), F32)] * 3
     for r in range(N_SEQ):
-        o2[r] = jnp.concatenate(run, 1)
+        o2[r] = jnp.concatenate(run, 1).astype(BF16)
         come = r1[r]
         run = [
             run[p] * come[p : p + 1, COLS:] + come[:, 128 * p : 128 * p + 128] for p in range(3)
@@ -398,6 +401,10 @@
 
     r2[s] = o2[s]
 
+    @pl.loop(6, ROWS // BLOCK)
+    def _(k):
+        inside(k)
+
     @pl.loop(0, ROWS // BLOCK)
     def _(k):
         row = pl.multiple_of(k * BLOCK, BLOCK)
@@ -408,8 +415,8 @@
         second_in(d).wait_recv()
 
     for j in range(N_SEQ):
-        ebuf[pl.ds(4 * j, 4), :] = r2[j]
-    entering = split(ebuf[...])
+        ebuf[pl.ds(4 * j, 4), :] = r2[j].astype(F32)
+    entering = ebuf[...].astype(BF16)
 
     def third(half, d):
         to = (e + d) % N_EXP
@@ -428,7 +435,7 @@
     for half in (0, 1):
         for k in (0, 2):
             at = pl.ds(512 * half + 128 * k, 2 * BLOCK)
-            far = dot3((cc[0, at, :], cc[1, at, :]), entering)
+            far = dot(cc[0, at, :], entering) + dot(cc[1, at, :], entering)
             gated = (ybuf[at, :] + ec[at, :] * far) * zg[at, :]
             ybuf[at, :] = gated
             gated = gated * gated
@@ -511,8 +518,8 @@
             pltpu.VMEM((8, 1, COLS), F32),
             pltpu.VMEM((N_SEQ, 4, COLS + 128), F32),
             pltpu.VMEM((N_SEQ, 4, COLS + 128), F32),
-            pltpu.VMEM((N_SEQ, 4, COLS), F32),
-            pltpu.VMEM((N_SEQ, 4, COLS), F32),
+            pltpu.VMEM((N_SEQ, 4, COLS), BF16),
+            pltpu.VMEM((N_SEQ, 4, COLS), BF16),
             pltpu.VMEM((STATE, COLS), F32),
             pltpu.VMEM((2, 4, 1, 128), F32),
             pltpu.VMEM((2, N_EXP, 4, 1, 128), F32),

time: 72.9 us -> 72 us (0.988)
  Pallas kernels: 70.7 us -> 69.8 us
    pallas_call x1, Pallas kernels: 70.7 us -> 69.8 us  [body(): pl.pallas_call(kernel, out_shape=jax.ShapeDtypeStruct((ROWS, COLS), BF16)...]
where the time goes in v3:
time: 72 us; the launch traced here: 71.9 us
  Pallas kernels  69.8 us (97%)
  local copies, waits for them, and re-layouts  2.09 us (3%)
    pallas_call x1, Pallas kernels, body(): pl.pallas_call(kernel, out_shape=jax.ShapeDtypeStruct((ROWS, COLS), BF16)...  69.8 us
    unnamed x1, local copies, waits for them, and re-layouts  2.09 us

profile of v3, /device:TPU:1, one launch (start us, length us, event | category | flops | bytes accessed | tf_op | source)
XLA Modules:
  0.0 71.9 jit_solution(1079901862234528463)
XLA Ops:
  0.0 69.8 %shard_map.145 = bf16[1024,384]{1,0:T(8,128)(2,1)} custom-call(bf16[128,2560]{1,0:T(8,128)(2,1)} %tok_hbm.1, s32[1,128]{1,0:T(1,128)} %bitcast.5, bf16[2560,2,384]{2,1,0:T(2,128)(2,1)} %wgi_hbm.1, bf16[2560,256]{1,0:T(8,128)(2,1)} %wbc_hbm.1, bf16[6,2560]{1,0:T(8,128)(2,1)} %bitcast.4, bf16[16,2560]{1,0:T(8,128)(2,1)} %bitcast.3, ...), custom_call_target="tpu_custom_call" | custom-call | tf_op jit(solution)/shard_map/pallas_call | solution.py:482
  69.8 2.1 %copy.17 = bf16[1024,384]{1,0:T(8,128)(2,1)} copy(bf16[1024,384]{1,0:T(8,128)(2,1)} %shard_map.145) | data formatting | bytes 1572864
